TPU v7x, 512 devices: a whole 4x8x8 slice. The times are simulated.
512 devices in a mesh: seq: 32 (over x_hi, y, core), doc: 16 (over x_lo, z).
Axes of the slice: x: 4 (x_hi: 2, x_lo: 2; x = x_hi * 2 + x_lo), y: 8, z: 8, core: 2. Of those that a mesh axis runs over, the one named last changes fastest.
Arguments:
- hidden: bfloat16 [16, 4096, 768], P('doc', 'seq'), may hold values from -3 to 3
- queries: bfloat16 [16, 4096, 768], P('doc', 'seq'), may hold values from -8 to 8
- key_states: bfloat16 [16, 4096, 768], P('doc', 'seq'), may hold values from -8 to 8
- values: bfloat16 [16, 4096, 768], P('doc', 'seq'), may hold values from -8 to 8
- targets: int32 [16, 4096], P('doc', 'seq'), may hold values from 0 to 26623
- lengths: int32 [16], replicated, may hold values from 2048 to 4096
- keep_rank: int32 [1], replicated, may hold values from 0 to 99
- out_weight: bfloat16 [768, 768], replicated, may hold values from -0.21875 to 0.21875
- final_gain: float32 [768], replicated, may hold values from 0.5 to 1.5
- unembed: bfloat16 [768, 26624], P(None, 'doc'), may hold values from -0.390625 to 0.390625
Outputs:
- token_nll: float32 [16, 4096], P('doc', 'seq')
- log_perplexity: float32 [16], replicated
- acceptance: float32 [16], replicated
All inputs are finite; a program needn't handle non-finite values.
Results may differ from a plain program's by a relative error of at most 0.007.
Values may be sent and summed in bfloat16 or wider, within the bound.
A program may use at most 64 MiB of HBM per device.

v0:
```python
import math
import jax
import jax.numpy as jnp
from jax import lax
from jax.sharding import Mesh
from jax.sharding import PartitionSpec as P

HEADS = 12
HEAD_DIM = 64
ROT = 16
DOC = ("doc_0", "doc_1")
NEGATIVE = -1e30
ROTARY_BASE = 10000.0
NORM_EPSILON = 1e-05
SPREAD_EPSILON = 0.0001


def in_order(blocks, dim):
    blocks = jnp.moveaxis(blocks, 0, dim)
    shape = blocks.shape
    return blocks.reshape(*shape[:dim], shape[dim] * shape[dim + 1], *shape[dim + 2 :])


def all_blocks(array, axes, turns):
    blocks = array[None]
    for k in turns:
        blocks = lax.all_gather(blocks, axes[k], axis=0, tiled=True)
    held = [lax.axis_size(axes[k]) for k in reversed(turns)]
    blocks = blocks.reshape(*held, *array.shape)
    turned = sorted(range(len(turns)), key=lambda place: turns[len(turns) - 1 - place])
    return blocks.transpose(*turned, *range(len(turns), blocks.ndim)).reshape(-1, *array.shape)


def gathered_by_axis(array, axes, turns, dim):
    return in_order(all_blocks(array, axes, turns), dim)


def from_everyone(array, axis):
    copies = jnp.broadcast_to(array, (lax.axis_size(axis), *array.shape))
    return lax.all_to_all(copies, axis, split_axis=0, concat_axis=0, tiled=True)


def collected_together(array, axis):
    leaves = jax.tree.leaves(array)
    turns = sorted(range(len(leaves)), key=lambda k: -leaves[k].size)
    width = (1, *leaves[turns[0]].shape)[-1]
    lines = [
        jnp.pad(leaves[k].reshape(-1), (0, -leaves[k].size % width)).reshape(-1, width)
        for k in turns
    ]
    both, at, found = (from_everyone(jnp.concatenate(lines), axis), 0, {})
    for k, line in zip(turns, lines):
        piece = both[:, at : at + len(line)].reshape(len(both), -1)
        found[k] = piece[:, : leaves[k].size].reshape(-1, *leaves[k].shape)
        at += len(line)
    numbers = iter(range(len(leaves)))
    return jax.tree.map(lambda _: found[next(numbers)], array)


def folded_in_pairs(pieces, combine):
    while len(jax.tree.leaves(pieces)[0]) > 1:
        pieces = jax.vmap(combine)(
            *(jax.tree.map(lambda part: part[side::2], pieces) for side in (0, 1))
        )
    return jax.tree.map(lambda part: part[0], pieces)


def joined_all(array, axis, combine):
    pieces = collected_together(array, axis)
    return folded_in_pairs(pieces, combine)


def over_copies(array, axis):
    everything = from_everyone(array, axis)
    return jnp.sum(everything, axis=0)


def rotate(block, first_row):
    row_count = block.shape[0]
    half_rot = ROT // 2
    where_at = (first_row + jnp.arange(row_count, dtype=jnp.int32)).astype(jnp.float32)
    inv_freq = ROTARY_BASE ** (
        -2.0 * jnp.arange(half_rot, dtype=jnp.int32).astype(jnp.float32) / ROT
    )
    angles = where_at[:, None] * inv_freq[None, :]
    cosine = jnp.cos(angles)[:, None, :]
    sine_part = jnp.sin(angles)[:, None, :]
    per_head = block.reshape(row_count, HEADS, HEAD_DIM)
    low_half = per_head[:, :, :half_rot]
    high_half = per_head[:, :, half_rot:ROT]
    turned = jnp.concatenate(
        [
            low_half * cosine - high_half * sine_part,
            high_half * cosine + low_half * sine_part,
            per_head[:, :, ROT:],
        ],
        axis=2,
    )
    return turned.reshape(row_count, HEADS * HEAD_DIM)


def combine(first_part, second_part):
    top_first, total_first, pick_first = first_part
    top_second, total_second, pick_second = second_part
    top_score = jnp.maximum(top_first, top_second)
    merged = total_first * jnp.exp(top_first - top_score) + total_second * jnp.exp(
        top_second - top_score
    )
    return (top_score, merged, pick_first + pick_second)


def accept(log_perplexity, keep_rank):
    doc_count = log_perplexity.shape[0]
    center = log_perplexity - jnp.mean(log_perplexity)
    spread = jnp.sqrt(jnp.mean(center * center) + SPREAD_EPSILON)
    ordered = jnp.sort(log_perplexity)
    scaled_rank = keep_rank[0] * (doc_count - 1)
    low_index = scaled_rank // 99
    high_index = jnp.minimum(low_index + 1, doc_count - 1)
    fraction = (scaled_rank - 99 * low_index).astype(jnp.float32) / 99.0
    places = jnp.arange(doc_count, dtype=jnp.int32)
    low_value = jnp.sum(jnp.where(places == low_index, ordered, 0.0))
    high_value = jnp.sum(jnp.where(places == high_index, ordered, 0.0))
    rank_level = (1.0 - fraction) * low_value + fraction * high_value
    return jax.nn.sigmoid((rank_level - log_perplexity) / spread)


def shards(
    hidden,
    queries,
    key_states,
    values,
    targets,
    lengths,
    keep_rank,
    out_weight,
    final_gain,
    unembed,
):
    tok_rows = queries.shape[1]
    seq_index = lax.axis_index("seq")
    first_row = seq_index * tok_rows
    turned_q = rotate(queries[0].astype(jnp.float32), first_row).astype(jnp.bfloat16)
    turned_k = rotate(key_states[0].astype(jnp.float32), first_row).astype(jnp.bfloat16)
    query_heads = turned_q.reshape(tok_rows, HEADS, HEAD_DIM)
    query_place = first_row + jnp.arange(tok_rows, dtype=jnp.int32)
    last_row = first_row + tok_rows - 1
    score_scale = 1.0 / math.sqrt(HEAD_DIM)
    key_value = jnp.stack([turned_k, values[0]])
    start_state = (
        jnp.full((HEADS, tok_rows), NEGATIVE, jnp.float32),
        jnp.zeros((HEADS, tok_rows), jnp.float32),
        jnp.zeros((HEADS, tok_rows, HEAD_DIM), jnp.float32),
    )

    def absorb(running, pair_block, begin_at):
        row_count = pair_block.shape[1]
        key_heads = pair_block[0].reshape(row_count, HEADS, HEAD_DIM)
        value_heads = pair_block[1].reshape(row_count, HEADS, HEAD_DIM)
        scores = (
            jnp.einsum("qhd,khd->hqk", query_heads, key_heads, preferred_element_type=jnp.float32)
            * score_scale
        )
        key_place = begin_at + jnp.arange(row_count, dtype=jnp.int32)
        allowed = key_place[None, None, :] <= query_place[None, :, None]
        scores = jnp.where(allowed, scores, NEGATIVE)
        old_top, totals, summed = running
        top_score = jnp.maximum(old_top, jnp.max(scores, axis=2))
        weights = jnp.where(allowed, jnp.exp(scores - top_score[:, :, None]), 0.0)
        factor = jnp.exp(old_top - top_score)
        totals = totals * factor + jnp.sum(weights, axis=2)
        summed = summed * factor[:, :, None] + jnp.einsum(
            "hqk,khd->hqd",
            weights.astype(jnp.bfloat16),
            value_heads,
            preferred_element_type=jnp.float32,
        )
        return (top_score, totals, summed)

    shard_piece = lax.all_gather(key_value, "seq", axis=1, tiled=True)
    row_count = shard_piece.shape[1]
    fold_block_rows = math.gcd(row_count, 512)

    def inner_step(block_index, inner_state):
        part_block = lax.dynamic_slice_in_dim(
            shard_piece, block_index * fold_block_rows, fold_block_rows, 1
        )
        block_begin = block_index * fold_block_rows
        return lax.cond(
            block_begin <= last_row,
            lambda state_now: absorb(state_now, part_block, block_begin),
            lambda state_now: state_now,
            inner_state,
        )

    running = lax.fori_loop(0, row_count // fold_block_rows, inner_step, start_state)
    top_final, total_final, summed_final = running
    attended = (
        jnp.transpose(summed_final / total_final[:, :, None], (1, 0, 2))
        .reshape(tok_rows, HEADS * HEAD_DIM)
        .astype(jnp.bfloat16)
    )
    residual = hidden[0].astype(jnp.float32) + jnp.dot(
        attended, out_weight, preferred_element_type=jnp.float32
    )
    center = residual - jnp.mean(residual, axis=1, keepdims=True)
    spread = jnp.mean(center * center, axis=1, keepdims=True)
    normed = (center * lax.rsqrt(spread + NORM_EPSILON) * final_gain).astype(jnp.bfloat16)
    gathered_rows, gathered_targets = (
        gathered_by_axis(normed[None], DOC, (0, 1), 0),
        gathered_by_axis(targets, DOC, (0, 1), 0),
    )
    doc_count = gathered_rows.shape[0]
    row_total = doc_count * tok_rows
    flat_rows = gathered_rows.reshape(row_total, HEADS * HEAD_DIM)
    flat_targets = gathered_targets.reshape(row_total)
    vocab_share = unembed.shape[1]
    doc_index = lax.axis_index(DOC)
    offset = doc_index * vocab_share
    block_rows = math.gcd(row_total, 512)

    def shard_stats(block_index):
        begin_at = block_index * block_rows
        block = lax.dynamic_slice_in_dim(flat_rows, begin_at, block_rows, 0)
        logits = jnp.dot(block, unembed, preferred_element_type=jnp.float32)
        top_score = jnp.max(logits, axis=1)
        totals = jnp.sum(jnp.exp(logits - top_score[:, None]), axis=1)
        wanted = lax.dynamic_slice_in_dim(flat_targets, begin_at, block_rows, 0) - offset
        matches = jnp.arange(vocab_share, dtype=jnp.int32)[None, :] == wanted[:, None]
        picked = jnp.sum(jnp.where(matches, logits, 0.0), axis=1)
        return (top_score, totals, picked)

    tops, totals, picks = lax.map(shard_stats, jnp.arange(row_total // block_rows, dtype=jnp.int32))
    tops = tops.reshape(doc_count, tok_rows)
    totals = totals.reshape(doc_count, tok_rows)
    picks = picks.reshape(doc_count, tok_rows)
    top_all, total_all, pick_all = joined_all((tops, totals, picks), DOC, combine)
    is_valid = query_place[None, :] < lengths[:, None]
    token_all = jnp.where(is_valid, top_all + jnp.log(total_all) - pick_all, 0.0)
    doc_sums = over_copies(jnp.sum(token_all, axis=1), "seq")
    log_perplexity = doc_sums / lengths.astype(jnp.float32)
    token_own = lax.dynamic_slice_in_dim(token_all, doc_index, 1, 0)
    acceptance = accept(log_perplexity, keep_rank)
    return (token_own, log_perplexity, acceptance)


def solution(mesh):
    split = Mesh(mesh.devices.reshape(mesh.shape["seq"], 2, 8), ("seq", "doc_0", "doc_1"))
    placed = (
        P(DOC, "seq", None),
        P(DOC, "seq", None),
        P(DOC, "seq", None),
        P(DOC, "seq", None),
        P(DOC, "seq"),
        P(),
        P(),
        P(),
        P(),
        P(None, DOC),
    )
    return jax.shard_map(
        shards, mesh=split, in_specs=placed, out_specs=(P(DOC, "seq"), P(), P()), check_vma=False
    )
```

profile of v0, /device:TPU:1, one launch (start us, length us, event | category | flops | bytes accessed | tf_op | source)
XLA Modules:
  0.0 322.7 jit_solution(12917053944295169730)
XLA Ops:
  7.2 1.2 copy.39
  8.5 1.1 copy.41
  9.6 1.1 copy.40
  10.9 0.8 pad_maximum_fusion
  11.8 140.8 %all-gather.8.cloned.1.call-done = bf16[2,4096,768]{1,2,0:T(8,128)(2,1)} async-done(((bf16[2,128,768]{1,2,0:T(8,128)(2,1)}), bf16[2,4096,768]{1,2,0:T(8,128)(2,1)}) %all-gather.8.cloned.1.call-update) | async-done | bytes 12582928 | tf_op jit(solution)/shard_map/all_gather | solution.py:180
  152.7 4.8 %while.33 = (s32[]{:T(128)}, f32[12,128]{1,0:T(8,128)S(1)}, f32[12,128]{1,0:T(8,128)S(1)}, f32[12,128,64]{1,2,0:T(8,128)S(1)}, s32[]{:T(128)}, /*index=5*/bf16[2...) while((s32[]{:T(128)}, f32[12,128]{1,0:T(8,128)S(1)}, ...), condition=%wide.region_5.6_spmd.clone, body=%wide.region_0.5_spmd.clone.sunk | while | flops 211816064 | bytes 15505717 | solution.py:196
  152.8 4.4 %conditional.3 = ((f32[12,128]{1,0:T(8,128)S(1)}, f32[12,128]{1,0:T(8,128)S(1)}, f32[12,128,64]{1,2,0:T(8,128)S(1)})) conditional(s32[]{:T(128)} %convert_element_type.107, (f32[12,128]{1,0:T(8,128)S(1)}, f32[12,128]{1,0:T(8,128)S(1)}, f32[12,128,64]{1,2,0:T(8,128)S(1)}) %tuple.89, (s32[]{:T(128)}, s32[]{:T(128)}, bf16[2,4096,768]{1,2,0:T(8,128)(2,1)}, ...), branch_computations={%region_1.0_spmd, %region_2.4_spmd} | conditional | flops 211816064 | bytes 15504990 | solution.py:189
  152.8 1.5 constant_dynamic-slice_fusion.1
  154.5 0.8 fusion.2
  155.3 0.7 fusion.4
  156.0 1.1 fusion.8
  158.5 7.0 %all-gather = bf16[256,768]{1,0:T(8,128)(2,1)} all-gather(bf16[128,768]{1,0:T(8,128)(2,1)S(1)} %multiply_convert_fusion), channel_id=2, replica_groups=mesh['seq'=32,'doc_0'=2,'doc_1'=8] {'doc_0'}, dimensions={0}, use_global_device_ids=true | all-gather | bytes 589824 | tf_op jit(solution)/shard_map/all_gather | solution.py:27
  165.5 3.1 all-gather.3
  168.6 13.5 %all-gather.4 = s32[8,2,128]{2,1,0:T(2,128)S(1)} all-gather(s32[1,2,128]{2,1,0:T(2,128)S(1)} %bitcast.81), channel_id=4, replica_groups=mesh['seq'=32,'doc_0'=2,'doc_1'=8] {'doc_1'}, dimensions={0}, use_global_device_ids=true | all-gather | bytes 9216 | tf_op jit(solution)/shard_map/all_gather | solution.py:27
  182.1 59.3 %all-gather.10.cloned.1.call-done = bf16[16,1,128,768]{3,2,1,0:T(8,128)(2,1)} async-done(((bf16[2,1,128,768]{3,2,1,0:T(8,128)(2,1)}), bf16[16,1,128,768]{3,2,1,0:T(8,128)(2,1)}) %all-gather.10.cloned.1.call-update) | async-done | bytes 3145744 | tf_op jit(solution)/shard_map/all_gather | solution.py:27
  241.4 3.9 %copy.43 = bf16[2,8,1,128,768]{4,3,1,0,2:T(8,128)(2,1)} copy(bf16[2,8,1,128,768]{4,3,0,1,2:T(8,128)(2,1)} %bitcast.69) | data formatting | bytes 6291456 | tf_op jit(solution)/shard_map/transpose | solution.py:31
  245.3 25.4 %while.32 = (s32[]{:T(128)}, f32[4,512]{1,0:T(4,128)S(1)}, f32[4,512]{1,0:T(4,128)S(1)}, f32[4,512]{1,0:T(4,128)S(1)}, s32[4]{0:T(128)S(1)}, /*index=5*/bf16[204...) while((s32[]{:T(128)}, f32[4,512]{1,0:T(4,128)S(1)}, ...), condition=%wide.region_12.13_spmd, body=%wide.region_8.12_spmd.sunk | while | flops 1313733632 | bytes 10184911 | solution.py:233
  246.5 3.7 %fusion.42 = (f32[512]{0:T(512)S(1)}, f32[512,1664]{1,0:T(8,128)S(1)}) fusion(bf16[768,1664]{1,0:T(8,128)(2,1)} %get-tuple-element.568, bf16[2048,768]{1,0:T(8,128)(2,1)} %get-tuple-element.567, s32[]{:T(128)S(6)} %select_n.101), kind=kOutput, calls=%fused_computation.76.clone.1 | convolution fusion | flops 1309474304 | bytes 6752260 | tf_op jit(solution)/shard_map/while/body/eval_jaxpr/dot_general | solution.py:225
  250.3 1.2 select_reduce_fusion.2
  252.9 3.7 %fusion.42 = (f32[512]{0:T(512)S(1)}, f32[512,1664]{1,0:T(8,128)S(1)}) fusion(bf16[768,1664]{1,0:T(8,128)(2,1)} %get-tuple-element.568, bf16[2048,768]{1,0:T(8,128)(2,1)} %get-tuple-element.567, s32[]{:T(128)S(6)} %select_n.101), kind=kOutput, calls=%fused_computation.76.clone.1 | convolution fusion | flops 1309474304 | bytes 6752260 | tf_op jit(solution)/shard_map/while/body/eval_jaxpr/dot_general | solution.py:225
  256.6 1.2 select_reduce_fusion.2
  259.2 3.7 %fusion.42 = (f32[512]{0:T(512)S(1)}, f32[512,1664]{1,0:T(8,128)S(1)}) fusion(bf16[768,1664]{1,0:T(8,128)(2,1)} %get-tuple-element.568, bf16[2048,768]{1,0:T(8,128)(2,1)} %get-tuple-element.567, s32[]{:T(128)S(6)} %select_n.101), kind=kOutput, calls=%fused_computation.76.clone.1 | convolution fusion | flops 1309474304 | bytes 6752260 | tf_op jit(solution)/shard_map/while/body/eval_jaxpr/dot_general | solution.py:225
  263.0 1.2 select_reduce_fusion.2
  265.6 3.7 %fusion.42 = (f32[512]{0:T(512)S(1)}, f32[512,1664]{1,0:T(8,128)S(1)}) fusion(bf16[768,1664]{1,0:T(8,128)(2,1)} %get-tuple-element.568, bf16[2048,768]{1,0:T(8,128)(2,1)} %get-tuple-element.567, s32[]{:T(128)S(6)} %select_n.101), kind=kOutput, calls=%fused_computation.76.clone.1 | convolution fusion | flops 1309474304 | bytes 6752260 | tf_op jit(solution)/shard_map/while/body/eval_jaxpr/dot_general | solution.py:225
  269.3 1.2 select_reduce_fusion.2
  270.8 0.8 broadcast_in_dim.91
  271.5 4.9 %all-to-all-start = ((f32[16,48,128]{2,1,0:T(8,128)}), f32[16,48,128]{2,1,0:T(8,128)S(1)}, u32[]{:S(2)}, u32[]{:S(2)}) async-start(f32[16,48,128]{2,1,0:T(8,128)} %broadcast_in_dim.91), calls=%async_computation | async-start | bytes 786432 | tf_op jit(solution)/shard_map/all_to_all | solution.py:40
  277.1 10.4 %all-to-all-done = f32[16,48,128]{2,1,0:T(8,128)S(1)} async-done(((f32[16,48,128]{2,1,0:T(8,128)}), f32[16,48,128]{2,1,0:T(8,128)S(1)}, u32[]{:S(2)}, u32[]{:S(2)}) %all-to-all-start) | async-done | bytes 393248 | tf_op jit(solution)/shard_map/all_to_all | solution.py:40
  288.4 11.5 %all-to-all-start.1 = ((f32[32,1,16]{2,1,0:T(1,128)}), f32[32,1,16]{2,1,0:T(1,128)S(1)}, u32[]{:S(2)}, u32[]{:S(2)}) async-start(f32[32,1,16]{2,1,0:T(1,128)} %broadcast_in_dim.93), calls=%async_computation.1 | async-start | bytes 32768 | tf_op jit(solution)/shard_map/all_to_all | solution.py:40
  300.5 8.9 %all-to-all-done.1 = f32[32,1,16]{2,1,0:T(1,128)S(1)} async-done(((f32[32,1,16]{2,1,0:T(1,128)}), f32[32,1,16]{2,1,0:T(1,128)S(1)}, u32[]{:S(2)}, u32[]{:S(2)}) %all-to-all-start.1) | async-done | bytes 2080 | tf_op jit(solution)/shard_map/all_to_all | solution.py:40
  310.0 1.4 sort.15
  311.4 0.7 fusion.25
  (100 shorter events, 8.1 us)
Async XLA Ops:
  7.2 150.5 %copy-start = (bf16[768,768]{1,0:T(8,128)(2,1)S(1)}, bf16[768,768]{1,0:T(8,128)(2,1)}, u32[]{:S(2)}) copy-start(bf16[768,768]{1,0:T(8,128)(2,1)} %param.23) | copy-start | bytes 3538948
  7.2 145.5 %all-gather.8.cloned.1.call-start = ((), (), s32[]{:S(2)}) async-start(), calls=%async_computation.2 | async-start | bytes 12976128 | tf_op jit(solution)/shard_map/all_gather | solution.py:180
  11.7 229.7 %all-gather.10.cloned.1.call-start = ((), (), s32[]{:S(2)}) async-start(), calls=%async_computation.3 | async-start | bytes 3538944 | tf_op jit(solution)/shard_map/all_gather | solution.py:27
  152.7 4.9 %copy-start.1 = (bf16[1,128,768]{2,1,0:T(8,128)(2,1)S(1)}, bf16[1,128,768]{2,1,0:T(8,128)(2,1)}, u32[]{:S(2)}) copy-start(bf16[1,128,768]{2,1,0:T(8,128)(2,1)} %param.16) | copy-start | bytes 589828
  152.7 5.6 %copy-start.2 = (f32[768]{0:T(1024)S(1)}, f32[768]{0:T(1024)}, u32[]{:S(2)}) copy-start(f32[768]{0:T(1024)} %param.24) | copy-start | bytes 9220
  157.6 7.9 %copy-start.5 = (s32[1,128]{1,0:T(1,128)S(1)}, s32[1,128]{1,0:T(1,128)}, u32[]{:S(2)}) copy-start(s32[1,128]{1,0:T(1,128)} %param.20) | copy-start | bytes 1540
  270.7 16.9 %copy-start.3 = (s32[16]{0:T(128)S(1)}, s32[16]{0:T(128)}, u32[]{:S(2)}) copy-start(s32[16]{0:T(128)} %param.21) | copy-start | bytes 196
  271.5 15.9 %all-to-all-start = ((f32[16,48,128]{2,1,0:T(8,128)}), f32[16,48,128]{2,1,0:T(8,128)S(1)}, u32[]{:S(2)}, u32[]{:S(2)}) async-start(f32[16,48,128]{2,1,0:T(8,128)} %broadcast_in_dim.91), calls=%async_computation | async-start | bytes 786432 | tf_op jit(solution)/shard_map/all_to_all | solution.py:40
  288.4 20.9 %all-to-all-start.1 = ((f32[32,1,16]{2,1,0:T(1,128)}), f32[32,1,16]{2,1,0:T(1,128)S(1)}, u32[]{:S(2)}, u32[]{:S(2)}) async-start(f32[32,1,16]{2,1,0:T(1,128)} %broadcast_in_dim.93), calls=%async_computation.1 | async-start | bytes 32768 | tf_op jit(solution)/shard_map/all_to_all | solution.py:40
  310.0 5.8 %copy-start.4 = (f32[16]{0:T(128)}, f32[16]{0:T(128)S(1)}, u32[]{:S(2)}) copy-start(f32[16]{0:T(128)S(1)} %get-tuple-element.352) | copy-start | bytes 196
Sparse Core Ops, SparseCore 0:
  11.9 140.7 all-gather.7
  165.6 75.8 all-gather.9
where the time goes:
time: 323 us
  waiting for transfers between devices  219 us (68%)
  blocking collectives  23.5 us (7%)
  between operations  17.7 us (5%)
  matrix products  17 us (5%)
  starting transfers between devices  16.5 us (5%)
  local copies, waits for them, and re-layouts  13.8 us (4%)
  other arithmetic  11.6 us (4%)
    all_gather x1, waiting for transfers between devices, shards(): shard_piece = lax.all_gather(key_value, 'seq', axis=1, tiled=True)  141 us
    all_gather x1, waiting for transfers between devices, all_blocks(): blocks = lax.all_gather(blocks, axes[k], axis=0, tiled=True)  59.3 us
    all_gather x3, blocking collectives, all_blocks(): blocks = lax.all_gather(blocks, axes[k], axis=0, tiled=True)  23.5 us
    all_to_all x2, waiting for transfers between devices, from_everyone(): return lax.all_to_all(copies, axis, split_axis=0, concat_axis=0, tiled=True)  19.3 us
    all_to_all x2, starting transfers between devices, from_everyone(): return lax.all_to_all(copies, axis, split_axis=0, concat_axis=0, tiled=True)  16.4 us
    dot_general x4, matrix products, shard_stats(): logits = jnp.dot(block, unembed, preferred_element_type=jnp.float32)  14.6 us
  transfers between devices with their start and end apart: 4, of which 4 were waited for; matrix products, arithmetic and copies ran while one was open for 0% of the time, Pallas kernels for 0%

commit v1 on v0

--- a/solution.py
+++ b/solution.py
@@ -24,7 +24,9 @@
 def all_blocks(array, axes, turns):
     blocks = array[None]
     for k in turns:
-        blocks = lax.all_gather(blocks, axes[k], axis=0, tiled=True)
+        blocks = jnp.concatenate(
+            lax.all_to_all(jnp.stack([blocks] * lax.axis_size(axes[k])), axes[k], 0, 0), axis=0
+        )
     held = [lax.axis_size(axes[k]) for k in reversed(turns)]
     blocks = blocks.reshape(*held, *array.shape)
     turned = sorted(range(len(turns)), key=lambda place: turns[len(turns) - 1 - place])

time: 323 us -> 357 us (1.11)
  starting transfers between devices: 16.5 us -> 61.7 us
  blocking collectives: 23.5 us -> 8.81 us
    all_to_all x0 -> x3, waiting for transfers between devices: none -> 77.3 us  [all_blocks(): lax.all_to_all(jnp.stack([blocks] * lax.axis_size(axes[k])), axes[k], 0, 0)]
    all_gather x1 -> x0, waiting for transfers between devices: 59.3 us -> none  [all_blocks(): blocks = lax.all_gather(blocks, axes[k], axis=0, tiled=True)]
    all_to_all x2, starting transfers between devices: 16.4 us -> 41 us  [from_everyone(): return lax.all_to_all(copies, axis, split_axis=0, concat_axis=0, tiled=True)]
    all_gather x3 -> x0, blocking collectives: 23.5 us -> none  [all_blocks(): blocks = lax.all_gather(blocks, axes[k], axis=0, tiled=True)]
    all_to_all x0 -> x3, starting transfers between devices: none -> 20.7 us  [all_blocks(): lax.all_to_all(jnp.stack([blocks] * lax.axis_size(axes[k])), axes[k], 0, 0)]
    all_gather x1, waiting for transfers between devices: 141 us -> 123 us  [shards(): shard_piece = lax.all_gather(key_value, 'seq', axis=1, tiled=True)]
    all_to_all x0 -> x1, blocking collectives: none -> 8.81 us  [all_blocks(): lax.all_to_all(jnp.stack([blocks] * lax.axis_size(axes[k])), axes[k], 0, 0)]
    all_to_all x0 -> x2, local copies, waits for them, and re-layouts: none -> 3.87 us  [all_blocks(): lax.all_to_all(jnp.stack([blocks] * lax.axis_size(axes[k])), axes[k], 0, 0)]
  transfers between devices with their start and end apart: 4 -> 6, of which waited for: 4 -> 5; matrix products, arithmetic and copies ran while one was open for 0% -> 2% of each run, Pallas kernels for 0% -> 0%
where the time goes in v1:
time: 357 us
  waiting for transfers between devices  220 us (62%)
  starting transfers between devices  61.7 us (17%)
  between operations  17.7 us (5%)
  matrix products  17 us (5%)
  local copies, waits for them, and re-layouts  16.4 us (5%)
  other arithmetic  12.2 us (3%)
  blocking collectives  8.81 us (2%)
    all_gather x1, waiting for transfers between devices, shards(): shard_piece = lax.all_gather(key_value, 'seq', axis=1, tiled=True)  123 us
    all_to_all x3, waiting for transfers between devices, all_blocks(): lax.all_to_all(jnp.stack([blocks] * lax.axis_size(axes[k])), axes[k], 0, 0)  77.3 us
    all_to_all x2, starting transfers between devices, from_everyone(): return lax.all_to_all(copies, axis, split_axis=0, concat_axis=0, tiled=True)  41 us
    all_to_all x3, starting transfers between devices, all_blocks(): lax.all_to_all(jnp.stack([blocks] * lax.axis_size(axes[k])), axes[k], 0, 0)  20.7 us
    all_to_all x2, waiting for transfers between devices, from_everyone(): return lax.all_to_all(copies, axis, split_axis=0, concat_axis=0, tiled=True)  19.3 us
    dot_general x4, matrix products, shard_stats(): logits = jnp.dot(block, unembed, preferred_element_type=jnp.float32)  14.6 us
    all_to_all x1, blocking collectives, all_blocks(): lax.all_to_all(jnp.stack([blocks] * lax.axis_size(axes[k])), axes[k], 0, 0)  8.81 us
  transfers between devices with their start and end apart: 6, of which 5 were waited for; matrix products, arithmetic and copies ran while one was open for 2% of the time, Pallas kernels for 0%

profile of v1, /device:TPU:1, one launch (start us, length us, event | category | flops | bytes accessed | tf_op | source)
XLA Modules:
  0.0 356.6 jit_solution(2756570905811912718)
XLA Ops:
  7.3 1.2 copy.39
  8.5 1.1 copy.41
  9.6 1.1 copy.40
  10.9 0.8 pad_maximum_fusion
  12.3 3.3 all-to-all-start.2
  15.7 3.0 all-to-all-done.2
  19.3 10.3 %all-to-all-start.3 = ((s32[8,2,1,128]{3,1,2,0:T(2,128)}), s32[8,2,1,128]{3,1,2,0:T(2,128)S(1)}, u32[]{:S(2)}, u32[]{:S(2)}) async-start(s32[8,2,1,128]{3,1,2,0:T(2,128)} %stack.20), calls=%async_computation.3 | async-start | bytes 16384 | tf_op jit(solution)/shard_map/all_to_all | solution.py:28
  29.6 123.1 %all-gather.2.cloned.1.call-done = bf16[2,4096,768]{1,2,0:T(8,128)(2,1)} async-done(((bf16[2,128,768]{1,2,0:T(8,128)(2,1)}), bf16[2,4096,768]{1,2,0:T(8,128)(2,1)}) %all-gather.2.cloned.1.call-update) | async-done | bytes 12582928 | tf_op jit(solution)/shard_map/all_gather | solution.py:182
  152.7 4.8 %while.33 = (s32[]{:T(128)}, f32[12,128]{1,0:T(8,128)S(1)}, f32[12,128]{1,0:T(8,128)S(1)}, f32[12,128,64]{1,2,0:T(8,128)S(1)}, s32[]{:T(128)}, /*index=5*/bf16[2...) while((s32[]{:T(128)}, f32[12,128]{1,0:T(8,128)S(1)}, ...), condition=%wide.region_5.6_spmd.clone, body=%wide.region_0.5_spmd.clone.sunk | while | flops 211816064 | bytes 15505717 | solution.py:198
  152.8 4.4 %conditional.3 = ((f32[12,128]{1,0:T(8,128)S(1)}, f32[12,128]{1,0:T(8,128)S(1)}, f32[12,128,64]{1,2,0:T(8,128)S(1)})) conditional(s32[]{:T(128)} %convert_element_type.109, (f32[12,128]{1,0:T(8,128)S(1)}, f32[12,128]{1,0:T(8,128)S(1)}, f32[12,128,64]{1,2,0:T(8,128)S(1)}) %tuple.89, (s32[]{:T(128)}, s32[]{:T(128)}, bf16[2,4096,768]{1,2,0:T(8,128)(2,1)}, ...), branch_computations={%region_1.0_spmd, %region_2.4_spmd} | conditional | flops 211816064 | bytes 15504990 | solution.py:191
  152.8 1.5 constant_dynamic-slice_fusion.1
  154.5 0.8 fusion.2
  156.0 1.1 fusion.8
  158.5 8.8 %all_to_all.31 = bf16[2,1,1,128,768]{4,3,2,1,0:T(8,128)(2,1)S(1)} all-to-all(bf16[2,1,1,128,768]{4,3,2,1,0:T(8,128)(2,1)S(1)} %pad_maximum_fusion.1), channel_id=1, replica_groups=mesh['seq'=32,'doc_0'=2,'doc_1'=8] {'doc_0'}, dimensions={0} | all-to-all | bytes 786432 | tf_op jit(solution)/shard_map/all_to_all | solution.py:28
  167.3 2.0 stack.18
  169.3 7.1 %all-to-all-start.1 = ((bf16[8,2,1,128,768]{4,3,1,2,0:T(8,128)(2,1)}), bf16[8,2,1,128,768]{4,3,1,2,0:T(8,128)(2,1)}, u32[]{:S(2)}, u32[]{:S(2)}) async-start(bf16[8,2,1,128,768]{4,3,1,2,0:T(8,128)(2,1)} %stack.18), calls=%async_computation.1 | async-start | bytes 6291456 | tf_op jit(solution)/shard_map/all_to_all | solution.py:28
  176.4 74.3 %all-to-all-done.1 = bf16[8,2,1,128,768]{4,3,1,2,0:T(8,128)(2,1)} async-done(((bf16[8,2,1,128,768]{4,3,1,2,0:T(8,128)(2,1)}), bf16[8,2,1,128,768]{4,3,1,2,0:T(8,128)(2,1)}, u32[]{:S(2)}, u32[]{:S(2)}) %all-to-all-start.1) | async-done | bytes 3145760 | tf_op jit(solution)/shard_map/all_to_all | solution.py:28
  250.7 3.9 %copy.42 = bf16[8,2,1,128,768]{4,3,0,1,2:T(8,128)(2,1)} copy(bf16[8,2,1,128,768]{4,3,1,2,0:T(8,128)(2,1)} %all-to-all-done.1) | data formatting | bytes 6291456 | tf_op jit(solution)/shard_map/all_to_all | solution.py:28
  254.6 25.4 %while.32 = (s32[]{:T(128)}, f32[4,512]{1,0:T(4,128)S(1)}, f32[4,512]{1,0:T(4,128)S(1)}, f32[4,512]{1,0:T(4,128)S(1)}, s32[4]{0:T(128)S(1)}, /*index=5*/bf16[204...) while((s32[]{:T(128)}, f32[4,512]{1,0:T(4,128)S(1)}, ...), condition=%wide.region_12.13_spmd, body=%wide.region_8.12_spmd.sunk | while | flops 1313733632 | bytes 10184911 | solution.py:235
  255.8 3.7 %fusion.43 = (f32[512]{0:T(512)S(1)}, f32[512,1664]{1,0:T(8,128)S(1)}) fusion(bf16[768,1664]{1,0:T(8,128)(2,1)} %get-tuple-element.568, bf16[2048,768]{1,0:T(8,128)(2,1)} %get-tuple-element.567, s32[]{:T(128)S(6)} %select_n.101), kind=kOutput, calls=%fused_computation.79.clone.1 | convolution fusion | flops 1309474304 | bytes 6752260 | tf_op jit(solution)/shard_map/while/body/eval_jaxpr/dot_general | solution.py:227
  259.6 1.2 select_reduce_fusion.2
  262.2 3.7 %fusion.43 = (f32[512]{0:T(512)S(1)}, f32[512,1664]{1,0:T(8,128)S(1)}) fusion(bf16[768,1664]{1,0:T(8,128)(2,1)} %get-tuple-element.568, bf16[2048,768]{1,0:T(8,128)(2,1)} %get-tuple-element.567, s32[]{:T(128)S(6)} %select_n.101), kind=kOutput, calls=%fused_computation.79.clone.1 | convolution fusion | flops 1309474304 | bytes 6752260 | tf_op jit(solution)/shard_map/while/body/eval_jaxpr/dot_general | solution.py:227
  265.9 1.2 select_reduce_fusion.2
  268.5 3.7 %fusion.43 = (f32[512]{0:T(512)S(1)}, f32[512,1664]{1,0:T(8,128)S(1)}) fusion(bf16[768,1664]{1,0:T(8,128)(2,1)} %get-tuple-element.568, bf16[2048,768]{1,0:T(8,128)(2,1)} %get-tuple-element.567, s32[]{:T(128)S(6)} %select_n.101), kind=kOutput, calls=%fused_computation.79.clone.1 | convolution fusion | flops 1309474304 | bytes 6752260 | tf_op jit(solution)/shard_map/while/body/eval_jaxpr/dot_general | solution.py:227
  272.3 1.2 select_reduce_fusion.2
  274.9 3.7 %fusion.43 = (f32[512]{0:T(512)S(1)}, f32[512,1664]{1,0:T(8,128)S(1)}) fusion(bf16[768,1664]{1,0:T(8,128)(2,1)} %get-tuple-element.568, bf16[2048,768]{1,0:T(8,128)(2,1)} %get-tuple-element.567, s32[]{:T(128)S(6)} %select_n.101), kind=kOutput, calls=%fused_computation.79.clone.1 | convolution fusion | flops 1309474304 | bytes 6752260 | tf_op jit(solution)/shard_map/while/body/eval_jaxpr/dot_general | solution.py:227
  278.6 1.2 select_reduce_fusion.2
  280.8 3.6 all-to-all-start.4
  285.1 10.5 %all-to-all-done.4 = f32[16,48,128]{2,1,0:T(8,128)S(1)} async-done(((f32[16,48,128]{2,1,0:T(8,128)}), f32[16,48,128]{2,1,0:T(8,128)S(1)}, u32[]{:S(2)}, u32[]{:S(2)}) %all-to-all-start.4) | async-done | bytes 393248 | tf_op jit(solution)/shard_map/all_to_all | solution.py:42
  296.5 37.4 %all-to-all-start.5 = ((f32[32,1,16]{2,1,0:T(1,128)}), f32[32,1,16]{2,1,0:T(1,128)S(1)}, u32[]{:S(2)}, u32[]{:S(2)}) async-start(f32[32,1,16]{2,1,0:T(1,128)} %broadcast_in_dim.89), calls=%async_computation.5 | async-start | bytes 32768 | tf_op jit(solution)/shard_map/all_to_all | solution.py:42
  334.5 8.9 %all-to-all-done.5 = f32[32,1,16]{2,1,0:T(1,128)S(1)} async-done(((f32[32,1,16]{2,1,0:T(1,128)}), f32[32,1,16]{2,1,0:T(1,128)S(1)}, u32[]{:S(2)}, u32[]{:S(2)}) %all-to-all-start.5) | async-done | bytes 2080 | tf_op jit(solution)/shard_map/all_to_all | solution.py:42
  344.0 1.4 sort.15
  (105 shorter events, 11.4 us)
Async XLA Ops:
  7.2 150.5 %copy-start = (bf16[768,768]{1,0:T(8,128)(2,1)S(1)}, bf16[768,768]{1,0:T(8,128)(2,1)}, u32[]{:S(2)}) copy-start(bf16[768,768]{1,0:T(8,128)(2,1)} %param.23) | copy-start | bytes 3538948
  7.2 4.6 %copy-start.5 = (s32[1,128]{1,0:T(1,128)S(1)}, s32[1,128]{1,0:T(1,128)}, u32[]{:S(2)}) copy-start(s32[1,128]{1,0:T(1,128)} %param.20) | copy-start | bytes 1540
  7.2 145.5 %all-gather.2.cloned.1.call-start = ((), (), s32[]{:S(2)}) async-start(), calls=%async_computation.6 | async-start | bytes 12976128 | tf_op jit(solution)/shard_map/all_gather | solution.py:182
  12.3 6.4 %all-to-all-start.2 = ((s32[2,1,1,128]{3,2,1,0:T(1,128)}), s32[2,1,1,128]{3,2,1,0:T(1,128)S(1)}, u32[]{:S(2)}, u32[]{:S(2)}) async-start(s32[2,1,1,128]{3,2,1,0:T(1,128)} %pad_add_fusion), calls=%async_computation.2 | async-start | bytes 2048 | tf_op jit(solution)/shard_map/all_to_all | solution.py:28
  19.3 139.2 %all-to-all-start.3 = ((s32[8,2,1,128]{3,1,2,0:T(2,128)}), s32[8,2,1,128]{3,1,2,0:T(2,128)S(1)}, u32[]{:S(2)}, u32[]{:S(2)}) async-start(s32[8,2,1,128]{3,1,2,0:T(2,128)} %stack.20), calls=%async_computation.3 | async-start | bytes 16384 | tf_op jit(solution)/shard_map/all_to_all | solution.py:28
  152.7 4.9 %copy-start.1 = (bf16[1,128,768]{2,1,0:T(8,128)(2,1)S(1)}, bf16[1,128,768]{2,1,0:T(8,128)(2,1)}, u32[]{:S(2)}) copy-start(bf16[1,128,768]{2,1,0:T(8,128)(2,1)} %param.16) | copy-start | bytes 589828
  152.7 5.6 %copy-start.2 = (f32[768]{0:T(1024)S(1)}, f32[768]{0:T(1024)}, u32[]{:S(2)}) copy-start(f32[768]{0:T(1024)} %param.24) | copy-start | bytes 9220
  169.3 81.4 %all-to-all-start.1 = ((bf16[8,2,1,128,768]{4,3,1,2,0:T(8,128)(2,1)}), bf16[8,2,1,128,768]{4,3,1,2,0:T(8,128)(2,1)}, u32[]{:S(2)}, u32[]{:S(2)}) async-start(bf16[8,2,1,128,768]{4,3,1,2,0:T(8,128)(2,1)} %stack.18), calls=%async_computation.1 | async-start | bytes 6291456 | tf_op jit(solution)/shard_map/all_to_all | solution.py:28
  280.0 15.7 %copy-start.3 = (s32[16]{0:T(128)S(1)}, s32[16]{0:T(128)}, u32[]{:S(2)}) copy-start(s32[16]{0:T(128)} %param.21) | copy-start | bytes 196
  280.8 14.7 %all-to-all-start.4 = ((f32[16,48,128]{2,1,0:T(8,128)}), f32[16,48,128]{2,1,0:T(8,128)S(1)}, u32[]{:S(2)}, u32[]{:S(2)}) async-start(f32[16,48,128]{2,1,0:T(8,128)} %broadcast_in_dim.87), calls=%async_computation.4 | async-start | bytes 786432 | tf_op jit(solution)/shard_map/all_to_all | solution.py:42
  296.5 46.8 %all-to-all-start.5 = ((f32[32,1,16]{2,1,0:T(1,128)}), f32[32,1,16]{2,1,0:T(1,128)S(1)}, u32[]{:S(2)}, u32[]{:S(2)}) async-start(f32[32,1,16]{2,1,0:T(1,128)} %broadcast_in_dim.89), calls=%async_computation.5 | async-start | bytes 32768 | tf_op jit(solution)/shard_map/all_to_all | solution.py:42
  344.0 5.8 %copy-start.4 = (f32[16]{0:T(128)}, f32[16]{0:T(128)S(1)}, u32[]{:S(2)}) copy-start(f32[16]{0:T(128)S(1)} %get-tuple-element.352) | copy-start | bytes 196
Sparse Core Ops, SparseCore 0:
  11.9 140.7 all-gather.1
